TPU v7x, 32 devices: a whole 2x2x4 slice. The times are simulated.
32 devices in a mesh: layer: 4 (over y, core), slab: 8 (over z, x).
Axes of the slice: x: 2, y: 2, z: 4, core: 2. Of those that a mesh axis runs over, the one named last changes fastest.
Arguments:
- weights: bfloat16 [8192, 16384], P('slab', 'layer'), may hold values from -0.29882812 to 0.29882812
- whitening: bfloat16 [8192, 8192], P('slab'), may hold values from -1 to 10, as said below
- test_matrix: int32 [16384, 1024], P(('layer', 'slab')), may hold values from -4 to 4
Outputs:
- basis: float32 [8192, 1024], P('slab')
- coefficients: float32 [16384, 1024], P('layer', 'slab')
Inputs may be any that keep to these rules, and one draw needn't show every extreme that they name: whitening is lower triangular with diagonal entries between 1 and 10.
All inputs are finite; a program needn't handle non-finite values.
Results may differ from a plain program's by a relative error of at most 0.006.
Values may be sent and summed in bfloat16 or wider, within the bound.
A program may use at most 128 MiB of HBM per device.

v0:
```python
import math
import jax
import jax.numpy as jnp
from jax import lax
from jax.sharding import PartitionSpec as P

D = 8192


def on_device(weights, whitening, test_matrix):
    rank_width = test_matrix.shape[1]
    slice_width = rank_width // lax.axis_size("layer")
    test_values = test_matrix.astype(jnp.bfloat16)
    columns = weights
    sketch_terms = jnp.dot(
        columns,
        lax.all_gather(test_values, "slab", axis=0, tiled=True),
        preferred_element_type=jnp.float32,
    )
    sketch = lax.psum_scatter(sketch_terms, "layer", scatter_dimension=1, tiled=True).astype(
        jnp.bfloat16
    )
    columns = whitening
    whitened_part = jnp.dot(
        columns,
        lax.all_gather(sketch, "slab", axis=0, tiled=True),
        preferred_element_type=jnp.float32,
    )
    whitened = lax.all_gather(whitened_part, "layer", axis=1, tiled=True)
    local_gram = jnp.dot(
        whitened.T, whitened, precision=lax.Precision.HIGHEST, preferred_element_type=jnp.float32
    )
    gram_matrix = lax.psum(local_gram, "slab")
    factor = jnp.linalg.cholesky(gram_matrix)
    ortho = jax.scipy.linalg.solve_triangular(factor, whitened.T, lower=True).T
    basis_half = ortho.astype(jnp.bfloat16)
    basis = basis_half.astype(jnp.float32) * math.sqrt(D)
    own_slice = lax.dynamic_slice_in_dim(
        basis_half, lax.axis_index("layer") * slice_width, slice_width, 1
    )
    columns = whitening
    projected_part = lax.psum_scatter(
        lax.dot_general(
            columns, own_slice, (((0,), (0,)), ((), ())), preferred_element_type=jnp.float32
        ),
        "slab",
        scatter_dimension=0,
        tiled=True,
    ).astype(jnp.bfloat16)
    projected = lax.all_gather(projected_part, "layer", axis=1, tiled=True)
    columns = weights
    coefficients = lax.psum_scatter(
        lax.dot_general(
            columns, projected, (((0,), (0,)), ((), ())), preferred_element_type=jnp.float32
        ),
        "slab",
        scatter_dimension=1,
        tiled=True,
    )
    return (basis, coefficients)


def solution(mesh):
    placed = (P("slab", "layer"), P("slab", None), P(("layer", "slab"), None))
    return jax.shard_map(
        on_device,
        mesh=mesh,
        in_specs=placed,
        out_specs=(P("slab", None), P("layer", "slab")),
        check_vma=False,
    )
```

profile of v0, /device:TPU:0, one launch (start us, length us, event | category | flops | bytes accessed | tf_op | source)
XLA Modules:
  0.0 1321.0 jit_solution(4433787939744664165)
XLA Ops:
  7.2 2.8 convert_element_type.15
  10.1 127.8 %all-gather.5.cloned.1.call-done = bf16[4096,1024]{1,0:T(8,128)(2,1)} async-done(((bf16[512,1024]{1,0:T(8,128)(2,1)}), bf16[4096,1024]{1,0:T(8,128)(2,1)}) %all-gather.5.cloned.1.call-update) | async-done | bytes 8388624 | tf_op jit(solution)/shard_map/all_gather | solution.py:17
  137.9 14.9 %fusion.73 = f32[1024,1024]{1,0:T(8,128)} fusion(bf16[1024,4096]{1,0:T(8,128)(2,1)} %param.3, bf16[4096,1024]{1,0:T(8,128)(2,1)} %all-gather.5.cloned.1.call-done), kind=kOutput, calls=%fused_computation.164 | convolution fusion | flops 8589934592 | bytes 20971520 | tf_op jit(solution)/shard_map/dot_general | solution.py:15
  152.9 42.7 %reduce-scatter.4.cloned.1.call-done = f32[1024,256]{1,0:T(8,128)} async-done(((f32[1024,1024]{1,0:T(8,128)}), f32[1024,256]{1,0:T(8,128)}) %reduce-scatter.4.cloned.1.call-update) | async-done | bytes 1048592 | tf_op jit(solution)/shard_map/reduce_scatter | solution.py:20
  195.6 2.1 convert_element_type.16
  197.8 73.4 %all-gather.7.cloned.1.call-done = bf16[8192,256]{1,0:T(8,128)(2,1)} async-done(((bf16[1024,256]{1,0:T(8,128)(2,1)}), bf16[8192,256]{1,0:T(8,128)(2,1)}) %all-gather.7.cloned.1.call-update) | async-done | bytes 4194320 | tf_op jit(solution)/shard_map/all_gather | solution.py:26
  271.1 12.6 convolution_bitcast_fusion.2
  284.0 32.9 %all-gather.9.cloned.1.call-done = f32[1024,1024]{0,1:T(8,128)} async-done(((f32[1024,256]{0,1:T(8,128)}), f32[1024,1024]{0,1:T(8,128)}) %all-gather.9.cloned.1.call-update) | async-done | bytes 4194320 | tf_op jit(solution)/shard_map/all_gather | solution.py:29
  316.9 18.2 %fusion.74 = f32[1024,1024]{0,1:T(8,128)} fusion(f32[1024,1024]{0,1:T(8,128)} %all-gather.9.cloned.1.call-done), kind=kOutput, calls=%fused_computation.165 | convolution fusion | flops 12884901888 | bytes 8388608 | tf_op jit(solution)/shard_map/dot_general | solution.py:30
  335.2 156.5 %all-reduce.3.cloned.1.call-done = f32[1024,1024]{0,1:T(8,128)} async-done(((f32[1024,1024]{0,1:T(8,128)}), f32[1024,1024]{0,1:T(8,128)}) %all-reduce.3.cloned.1.call-update) | async-done | bytes 4194320 | tf_op jit(solution)/shard_map/psum | solution.py:33
  491.6 5.7 copy.6
  497.4 4.4 fusion
  501.8 2.0 copy-done
  503.8 11.7 cholesky.223
  515.5 9.8 custom-call.63
  525.4 2.5 cholesky.255
  527.9 2.3 constant_dynamic-update-slice_fusion.25
  531.8 11.9 cholesky.244
  544.3 9.8 custom-call.64
  555.3 2.1 convolution_subtract_fusion.6
  557.4 11.7 cholesky.468
  570.4 9.8 custom-call.65
  581.3 2.3 convolution_subtract_fusion.7
  583.7 11.9 cholesky.487
  596.9 9.8 custom-call.66
  607.8 2.3 convolution_subtract_fusion.8
  610.1 11.7 cholesky.506
  623.1 10.2 custom-call.67
  634.3 2.3 convolution_subtract_fusion.9
  636.6 11.7 cholesky.526
  649.6 9.8 custom-call.68
  660.3 2.0 convolution_subtract_fusion.10
  662.4 11.9 cholesky.546
  675.5 9.8 custom-call.69
  686.2 1.8 convolution_subtract_fusion.11
  688.0 11.7 cholesky.564
  706.5 4.9 select_select_fusion
  711.4 22.8 %while.1 = (s32[]{:T(128)}, f32[1024,1024]{1,0:T(8,128)}, s32[8,2]{0,1:T(2,128)S(1)}, f32[8,128,128]{2,1,0:T(8,128)S(1)}, s32[]{:T(128)}) while((s32[]{:T(128)}, f32[1024,1024]{1,0:T(8,128)}, s32[8,2]{0,1:T(2,128)S(1)}, f32[8,128,128]{2,1,0:T(8,128)S(1)}, s32[]{:T(128)}) %tuple.58), condition=%wide.while_cond, body=%wide.while_body.sunk | while | flops 2 | bytes 131181 | solution.py:35
  712.0 2.2 bitcast_dynamic-update-slice_fusion.2
  714.9 2.2 bitcast_dynamic-update-slice_fusion.2
  717.8 2.2 bitcast_dynamic-update-slice_fusion.2
  720.6 2.2 bitcast_dynamic-update-slice_fusion.2
  723.5 2.2 bitcast_dynamic-update-slice_fusion.2
  726.3 2.2 bitcast_dynamic-update-slice_fusion.2
  729.2 2.2 bitcast_dynamic-update-slice_fusion.2
  732.1 2.2 bitcast_dynamic-update-slice_fusion.2
  734.2 78.8 %custom-call.70 = f32[8,128,128]{1,2,0:T(8,128)S(1)} custom-call(f32[8,128,128]{2,1,0:T(8,128)S(1)} %get-tuple-element.9), custom_call_target="InvertDiagBlocksLowerTriangular" | custom-call | tf_op jit(solution)/shard_map/jit(_solve_triangular)/triangular_solve | solution.py:35
  813.1 1.8 convert_dynamic-update-slice_fusion.6
  815.0 1.7 convolution_subtract_fusion.4
  817.4 1.6 convolution_subtract_fusion
  819.6 2.0 fusion.15
  822.3 2.4 fusion.18
  826.0 2.9 convolution_subtract_fusion.2
  829.7 3.0 convolution_subtract_fusion.1
  833.4 3.5 convolution_subtract_fusion.3
  837.6 6.7 convolution_bitcast_fusion
  844.3 147.0 %reduce-scatter.6.cloned.1.call-done = f32[1024,256]{0,1:T(8,128)} async-done(((f32[8192,256]{0,1:T(8,128)}), f32[1024,256]{0,1:T(8,128)}) %reduce-scatter.6.cloned.1.call-update) | async-done | bytes 1048592 | tf_op jit(solution)/shard_map/reduce_scatter | solution.py:42
  991.3 2.1 convert_element_type.18
  993.5 21.8 %all-gather.11.cloned.1.call-done = bf16[1024,1024]{0,1:T(8,128)(2,1)} async-done(((bf16[1024,256]{0,1:T(8,128)(2,1)}), bf16[1024,1024]{0,1:T(8,128)(2,1)}) %all-gather.11.cloned.1.call-update) | async-done | bytes 2097168 | tf_op jit(solution)/shard_map/all_gather | solution.py:50
  1015.2 16.0 %convolution_bitcast_fusion.1 = f32[4096,1024]{0,1:T(8,128)} fusion(bf16[1024,1024]{0,1:T(8,128)(2,1)} %all-gather.11.cloned.1.call-done, bf16[1024,4096]{1,0:T(8,128)(2,1)} %param.3), kind=kOutput, calls=%fused_computation.3 | convolution fusion | flops 8589934592 | bytes 27262976 | tf_op jit(solution)/shard_map/dot_general | solution.py:53
  1031.2 2.5 multiply_bitcast_fusion
  1033.7 5.3 copy.7
  1039.1 271.7 %reduce-scatter.8.cloned.1.call-done = f32[4096,128]{0,1:T(8,128)} async-done(((f32[4096,1024]{0,1:T(8,128)}), f32[4096,128]{0,1:T(8,128)}) %reduce-scatter.8.cloned.1.call-update) | async-done | bytes 2097168 | tf_op jit(solution)/shard_map/reduce_scatter | solution.py:52
  1310.8 2.9 copy.8
  (90 shorter events, 27.8 us)
Async XLA Ops:
  7.2 130.7 %all-gather.5.cloned.1.call-start = ((), (), s32[]{:S(2)}) async-start(), calls=%async_computation.3 | async-start | bytes 9437184 | tf_op jit(solution)/shard_map/all_gather | solution.py:17
  10.0 185.6 %reduce-scatter.4.cloned.1.call-start = ((), (), s32[]{:S(2)}) async-start(), calls=%async_computation.4 | async-start | bytes 5242880 | tf_op jit(solution)/shard_map/reduce_scatter | solution.py:20
  152.9 118.3 %all-gather.7.cloned.1.call-start = ((), (), s32[]{:S(2)}) async-start(), calls=%async_computation.5 | async-start | bytes 4718592 | tf_op jit(solution)/shard_map/all_gather | solution.py:26
  197.7 119.2 %all-gather.9.cloned.1.call-start = ((), (), s32[]{:S(2)}) async-start(), calls=%async_computation.6 | async-start | bytes 5242880 | tf_op jit(solution)/shard_map/all_gather | solution.py:29
  283.7 207.9 %all-reduce.3.cloned.1.call-start = ((), (), s32[]{:S(2)}) async-start(), calls=%async_computation.7 | async-start | bytes 8388608 | tf_op jit(solution)/shard_map/psum | solution.py:33
  335.1 656.2 %reduce-scatter.6.cloned.1.call-start = ((), (), s32[]{:S(2)}) async-start(), calls=%async_computation.8 | async-start | bytes 9437184 | tf_op jit(solution)/shard_map/reduce_scatter | solution.py:42
  501.8 2.0 copy-start
  813.1 4.3 copy-start.1
  822.3 15.2 %slice-start = ((s8[16777216]{0:T(1024)(128)(4,1)}), s8[4194304]{0:T(1024)(128)(4,1)S(1)}, s32[]{:S(2)}) async-start(s8[16777216]{0:T(1024)(128)(4,1)} %bitcast.119), calls=%async_computation.11 | async-start | bytes 8388608
  825.5 12.0 slice-start.1
  826.0 11.6 slice-start.2
  829.7 7.9 slice-start.3
  844.3 171.0 %all-gather.11.cloned.1.call-start = ((), (), s32[]{:S(2)}) async-start(), calls=%async_computation.9 | async-start | bytes 2621440 | tf_op jit(solution)/shard_map/all_gather | solution.py:50
  993.4 317.4 %reduce-scatter.8.cloned.1.call-start = ((), (), s32[]{:S(2)}) async-start(), calls=%async_computation.10 | async-start | bytes 18874368 | tf_op jit(solution)/shard_map/reduce_scatter | solution.py:52
Sparse Core Ops, SparseCore 0:
  10.7 127.1 all-gather.4
  153.0 42.5 reduce-scatter.3
  198.3 72.7 all-gather.6
  283.9 32.9 all-gather.8
  335.2 156.3 all-reduce.2
  844.4 146.8 reduce-scatter.5
  993.5 21.6 all-gather.10
  1031.3 279.4 reduce-scatter.7
where the time goes:
time: 1330 us; the launch traced here: 1320 us
  waiting for transfers between devices  874 us (66%)
  other arithmetic  270 us (20%)
  matrix products  115 us (9%)
  local copies, waits for them, and re-layouts  42.1 us (3%)
  between operations  19.9 us (1%)
    reduce_scatter x1, waiting for transfers between devices, on_device(): lax.psum_scatter(lax.dot_general(columns, projected, (((0,), (0,)), ((),...  272 us
    another operation x30, other arithmetic, on_device(): factor = jnp.linalg.cholesky(gram_matrix)  172 us
    psum x1, waiting for transfers between devices, on_device(): gram_matrix = lax.psum(local_gram, 'slab')  156 us
    reduce_scatter x1, waiting for transfers between devices, on_device(): lax.psum_scatter(lax.dot_general(columns, own_slice, (((0,), (0,)), ((),...  147 us
    all_gather x1, waiting for transfers between devices, on_device(): lax.all_gather(test_values, 'slab', axis=0, tiled=True)  128 us
    another operation x3, other arithmetic, on_device(): ortho = jax.scipy.linalg.solve_triangular(factor, whitened.T, lower=True).T  83.7 us
    all_gather x1, waiting for transfers between devices, on_device(): lax.all_gather(sketch, 'slab', axis=0, tiled=True)  73.4 us
    reduce_scatter x1, waiting for transfers between devices, on_device(): lax.psum_scatter(sketch_terms, 'layer', scatter_dimension=1, tiled=True)  42.7 us
  transfers between devices with their start and end apart: 8, of which 8 were waited for; matrix products, arithmetic and copies ran while one was open for 1% of the time, Pallas kernels for 0%

commit v1 on v0

--- a/solution.py
+++ b/solution.py
@@ -30,7 +30,7 @@
     local_gram = jnp.dot(
         whitened.T, whitened, precision=lax.Precision.HIGHEST, preferred_element_type=jnp.float32
     )
-    gram_matrix = lax.psum(local_gram, "slab")
+    gram_matrix = jnp.sum(lax.all_gather(local_gram, "slab"), axis=0)
     factor = jnp.linalg.cholesky(gram_matrix)
     ortho = jax.scipy.linalg.solve_triangular(factor, whitened.T, lower=True).T
     basis_half = ortho.astype(jnp.bfloat16)

time: 1330 us -> 1830 us (1.38)
  waiting for transfers between devices: 874 us -> 1360 us
    all_gather x0 -> x1, waiting for transfers between devices: none -> 638 us  [on_device(): gram_matrix = jnp.sum(lax.all_gather(local_gram, 'slab'), axis=0)]
    psum x1 -> x0, waiting for transfers between devices: 156 us -> none  [on_device(): gram_matrix = lax.psum(local_gram, 'slab')]
  transfers between devices with their start and end apart: 8 -> 8, of which waited for: 8 -> 8; matrix products, arithmetic and copies ran while one was open for 1% -> 0% of each run, Pallas kernels for 0% -> 0%
where the time goes in v1:
time: 1830 us; the launch traced here: 1820 us
  waiting for transfers between devices  1360 us (74%)
  other arithmetic  285 us (16%)
  matrix products  114 us (6%)
  local copies, waits for them, and re-layouts  42.7 us (2%)
  between operations  20 us (1%)
    all_gather x1, waiting for transfers between devices, on_device(): gram_matrix = jnp.sum(lax.all_gather(local_gram, 'slab'), axis=0)  638 us
    reduce_scatter x1, waiting for transfers between devices, on_device(): lax.psum_scatter(lax.dot_general(columns, projected, (((0,), (0,)), ((),...  272 us
    another operation x30, other arithmetic, on_device(): factor = jnp.linalg.cholesky(gram_matrix)  172 us
    reduce_scatter x1, waiting for transfers between devices, on_device(): lax.psum_scatter(lax.dot_general(columns, own_slice, (((0,), (0,)), ((),...  148 us
    all_gather x1, waiting for transfers between devices, on_device(): lax.all_gather(test_values, 'slab', axis=0, tiled=True)  128 us
    another operation x3, other arithmetic, on_device(): ortho = jax.scipy.linalg.solve_triangular(factor, whitened.T, lower=True).T  83.7 us
    all_gather x1, waiting for transfers between devices, on_device(): lax.all_gather(sketch, 'slab', axis=0, tiled=True)  73.4 us
    reduce_scatter x1, waiting for transfers between devices, on_device(): lax.psum_scatter(sketch_terms, 'layer', scatter_dimension=1, tiled=True)  42.7 us
  transfers between devices with their start and end apart: 8, of which 8 were waited for; matrix products, arithmetic and copies ran while one was open for 0% of the time, Pallas kernels for 0%

profile of v1, /device:TPU:0, one launch (start us, length us, event | category | flops | bytes accessed | tf_op | source)
XLA Modules:
  0.0 1818.6 jit_solution(10148576735818353473)
XLA Ops:
  7.2 2.8 convert_element_type.15
  10.1 127.8 %all-gather.7.cloned.1.call-done = bf16[4096,1024]{1,0:T(8,128)(2,1)} async-done(((bf16[512,1024]{1,0:T(8,128)(2,1)}), bf16[4096,1024]{1,0:T(8,128)(2,1)}) %all-gather.7.cloned.1.call-update) | async-done | bytes 8388624 | tf_op jit(solution)/shard_map/all_gather | solution.py:17
  137.9 14.9 fusion.73
  152.9 42.7 %reduce-scatter.4.cloned.1.call-done = f32[1024,256]{1,0:T(8,128)} async-done(((f32[1024,1024]{1,0:T(8,128)}), f32[1024,256]{1,0:T(8,128)}) %reduce-scatter.4.cloned.1.call-update) | async-done | bytes 1048592 | tf_op jit(solution)/shard_map/reduce_scatter | solution.py:20
  195.6 2.1 convert_element_type.16
  197.8 73.4 %all-gather.9.cloned.1.call-done = bf16[8192,256]{1,0:T(8,128)(2,1)} async-done(((bf16[1024,256]{1,0:T(8,128)(2,1)}), bf16[8192,256]{1,0:T(8,128)(2,1)}) %all-gather.9.cloned.1.call-update) | async-done | bytes 4194320 | tf_op jit(solution)/shard_map/all_gather | solution.py:26
  271.1 12.6 convolution_bitcast_fusion.2
  284.0 32.9 %all-gather.11.cloned.1.call-done = f32[1024,1024]{0,1:T(8,128)} async-done(((f32[1024,256]{0,1:T(8,128)}), f32[1024,1024]{0,1:T(8,128)}) %all-gather.11.cloned.1.call-update) | async-done | bytes 4194320 | tf_op jit(solution)/shard_map/all_gather | solution.py:29
  316.9 18.1 fusion.74
  335.1 637.7 %all-gather.15.cloned.1.call-done = f32[8192,1024]{1,0:T(8,128)} async-done(((f32[1024,1024]{1,0:T(8,128)}), f32[8192,1024]{1,0:T(8,128)}) %all-gather.15.cloned.1.call-update) | async-done | bytes 33554448 | tf_op jit(solution)/shard_map/all_gather | solution.py:33
  972.8 14.7 reduce_sum.9
  987.5 5.7 copy.8
  993.2 4.4 fusion
  997.7 1.9 copy-done
  999.6 11.7 cholesky.223
  1011.3 2.5 cholesky.255
  1013.9 9.8 custom-call.63
  1023.7 2.3 constant_dynamic-update-slice_fusion.25
  1027.6 11.9 cholesky.244
  1040.1 9.8 custom-call.64
  1051.1 2.1 convolution_subtract_fusion.6
  1053.2 11.7 cholesky.468
  1066.2 9.8 custom-call.65
  1077.2 2.3 convolution_subtract_fusion.7
  1079.5 11.9 cholesky.487
  1092.7 9.8 custom-call.66
  1103.6 2.3 convolution_subtract_fusion.8
  1105.9 11.7 cholesky.506
  1119.0 10.2 custom-call.67
  1130.2 2.3 convolution_subtract_fusion.9
  1132.5 11.7 cholesky.526
  1145.5 9.8 custom-call.68
  1156.2 2.0 convolution_subtract_fusion.10
  1158.3 11.9 cholesky.546
  1171.4 9.8 custom-call.69
  1182.1 1.8 convolution_subtract_fusion.11
  1183.9 11.7 cholesky.564
  1202.5 4.9 select_select_fusion
  1207.4 23.5 %while.1 = (s32[]{:T(128)}, f32[1024,1024]{1,0:T(8,128)}, s32[8,2]{0,1:T(2,128)S(1)}, f32[8,128,128]{2,1,0:T(8,128)S(1)}, s32[]{:T(128)}) while((s32[]{:T(128)}, f32[1024,1024]{1,0:T(8,128)}, s32[8,2]{0,1:T(2,128)S(1)}, f32[8,128,128]{2,1,0:T(8,128)S(1)}, s32[]{:T(128)}) %tuple.59), condition=%wide.while_cond, body=%wide.while_body.sunk | while | flops 2 | bytes 131181 | solution.py:35
  1208.1 2.2 bitcast_dynamic-update-slice_fusion.2
  1211.0 2.2 bitcast_dynamic-update-slice_fusion.2
  1214.0 2.2 bitcast_dynamic-update-slice_fusion.2
  1216.9 2.2 bitcast_dynamic-update-slice_fusion.2
  1219.8 2.2 bitcast_dynamic-update-slice_fusion.2
  1222.8 2.2 bitcast_dynamic-update-slice_fusion.2
  1225.7 2.2 bitcast_dynamic-update-slice_fusion.2
  1228.7 2.2 bitcast_dynamic-update-slice_fusion.2
  1230.9 78.8 %custom-call.70 = f32[8,128,128]{1,2,0:T(8,128)S(1)} custom-call(f32[8,128,128]{2,1,0:T(8,128)S(1)} %get-tuple-element.9), custom_call_target="InvertDiagBlocksLowerTriangular" | custom-call | tf_op jit(solution)/shard_map/jit(_solve_triangular)/triangular_solve | solution.py:35
  1309.7 1.8 convert_dynamic-update-slice_fusion.6
  1311.7 1.7 convolution_subtract_fusion.4
  1316.3 2.0 fusion.15
  1319.0 2.4 fusion.18
  1322.7 2.9 convolution_subtract_fusion.2
  1326.3 3.0 convolution_subtract_fusion.1
  1330.0 3.5 convolution_subtract_fusion.3
  1334.2 6.7 convolution_bitcast_fusion
  1341.0 147.9 %reduce-scatter.6.cloned.1.call-done = f32[1024,256]{0,1:T(8,128)} async-done(((f32[8192,256]{0,1:T(8,128)}), f32[1024,256]{0,1:T(8,128)}) %reduce-scatter.6.cloned.1.call-update) | async-done | bytes 1048592 | tf_op jit(solution)/shard_map/reduce_scatter | solution.py:42
  1488.9 2.1 convert_element_type.18
  1491.1 21.8 %all-gather.13.cloned.1.call-done = bf16[1024,1024]{0,1:T(8,128)(2,1)} async-done(((bf16[1024,256]{0,1:T(8,128)(2,1)}), bf16[1024,1024]{0,1:T(8,128)(2,1)}) %all-gather.13.cloned.1.call-update) | async-done | bytes 2097168 | tf_op jit(solution)/shard_map/all_gather | solution.py:50
  1512.8 16.0 convolution_bitcast_fusion.1
  1528.8 2.5 multiply_bitcast_fusion
  1531.4 5.3 copy.9
  1536.7 271.7 %reduce-scatter.8.cloned.1.call-done = f32[4096,128]{0,1:T(8,128)} async-done(((f32[4096,1024]{0,1:T(8,128)}), f32[4096,128]{0,1:T(8,128)}) %reduce-scatter.8.cloned.1.call-update) | async-done | bytes 2097168 | tf_op jit(solution)/shard_map/reduce_scatter | solution.py:52
  1808.4 2.9 copy.10
  (91 shorter events, 30.0 us)
Async XLA Ops:
  7.2 130.7 %all-gather.7.cloned.1.call-start = ((), (), s32[]{:S(2)}) async-start(), calls=%async_computation.3 | async-start | bytes 9437184 | tf_op jit(solution)/shard_map/all_gather | solution.py:17
  10.0 185.6 %reduce-scatter.4.cloned.1.call-start = ((), (), s32[]{:S(2)}) async-start(), calls=%async_computation.4 | async-start | bytes 5242880 | tf_op jit(solution)/shard_map/reduce_scatter | solution.py:20
  152.9 118.3 %all-gather.9.cloned.1.call-start = ((), (), s32[]{:S(2)}) async-start(), calls=%async_computation.5 | async-start | bytes 4718592 | tf_op jit(solution)/shard_map/all_gather | solution.py:26
  197.7 119.2 %all-gather.11.cloned.1.call-start = ((), (), s32[]{:S(2)}) async-start(), calls=%async_computation.6 | async-start | bytes 5242880 | tf_op jit(solution)/shard_map/all_gather | solution.py:29
  283.7 689.1 %all-gather.15.cloned.1.call-start = ((), (), s32[]{:S(2)}) async-start(), calls=%async_computation.10 | async-start | bytes 37748736 | tf_op jit(solution)/shard_map/all_gather | solution.py:33
  335.0 1153.9 %reduce-scatter.6.cloned.1.call-start = ((), (), s32[]{:S(2)}) async-start(), calls=%async_computation.7 | async-start | bytes 9437184 | tf_op jit(solution)/shard_map/reduce_scatter | solution.py:42
  997.7 1.9 copy-start
  1309.7 4.3 copy-start.1
  1319.0 15.2 slice-start
  1322.2 12.0 slice-start.1
  1322.6 11.5 slice-start.2
  1326.3 7.9 slice-start.3
  1340.9 171.9 %all-gather.13.cloned.1.call-start = ((), (), s32[]{:S(2)}) async-start(), calls=%async_computation.8 | async-start | bytes 2621440 | tf_op jit(solution)/shard_map/all_gather | solution.py:50
  1491.0 317.4 %reduce-scatter.8.cloned.1.call-start = ((), (), s32[]{:S(2)}) async-start(), calls=%async_computation.9 | async-start | bytes 18874368 | tf_op jit(solution)/shard_map/reduce_scatter | solution.py:52
Sparse Core Ops, SparseCore 0:
  10.7 127.1 all-gather.6
  153.0 42.5 reduce-scatter.3
  198.3 72.7 all-gather.8
  283.9 32.9 all-gather.10
  335.1 637.6 all-gather.14
  1341.0 147.8 reduce-scatter.5
  1491.1 21.6 all-gather.12
  1528.9 279.4 reduce-scatter.7
